TPU v7x, 128 devices: a whole 4x4x4 slice. The times are simulated.
128 devices in a mesh: shard: 16 (over z_hi, x, core), tp: 8 (over z_lo, y).
Axes of the slice: x: 4, y: 4, z: 4 (z_hi: 2, z_lo: 2; z = z_hi * 2 + z_lo), core: 2. Of those that a mesh axis runs over, the one named last changes fastest.
Arguments:
- train_query: bfloat16 [5120, 8192], P('shard', 'tp'), may hold values from -0.078125 to 0.078125
- low_query: bfloat16 [5120, 32], P('shard'), may hold values from -0.078125 to 0.078125
- high_query: bfloat16 [32, 8192], P(None, 'tp'), may hold values from -1 to 1
- train_key: bfloat16 [5120, 1024], P('shard', 'tp'), may hold values from -0.078125 to 0.078125
- low_key: bfloat16 [5120, 32], P('shard'), may hold values from -0.078125 to 0.078125
- high_key: bfloat16 [32, 1024], P(None, 'tp'), may hold values from -1 to 1
- train_value: bfloat16 [5120, 1024], P('shard', 'tp'), may hold values from -0.078125 to 0.078125
- low_value: bfloat16 [5120, 32], P('shard'), may hold values from -0.078125 to 0.078125
- high_value: bfloat16 [32, 1024], P(None, 'tp'), may hold values from -1 to 1
- train_mixed: bfloat16 [8192, 5120], P('tp', 'shard'), may hold values from -0.0625 to 0.0625
- low_mixed: bfloat16 [8192, 32], P('tp'), may hold values from -0.0625 to 0.0625
- high_mixed: bfloat16 [32, 5120], P(None, 'shard'), may hold values from -1 to 1
- norm_train: float32 [5120], P(('shard', 'tp')), may hold values from 0.25 to 1.75
- norm_step: float32 [5120], P(('shard', 'tp')), may hold values from -0.3 to 0.3
Outputs:
- final_query: bfloat16 [5120, 8192], P(None, 'tp')
- final_key: bfloat16 [5120, 1024], P(None, 'tp')
- final_value: bfloat16 [5120, 1024], P(None, 'tp')
- final_mixed: bfloat16 [8192, 5120], P('tp')
- serve_norm: bfloat16 [5120], replicated
All inputs are finite; a program needn't handle non-finite values.
Results may differ from a plain program's by a relative error of at most 0.001.
Values may be sent and summed in bfloat16 or wider, within the bound.
A program may use at most 128 MiB of HBM per device.

v0:
```python
import jax
import jax.numpy as jnp
from jax import lax
from jax.sharding import PartitionSpec as P

mix_rate = 0.5


def rows_first(arrays, axis, dims):
    turned = [jnp.moveaxis(a, dim, 0) for a, dim in zip(arrays, dims)]
    widths = [t[0].size for t in turned]
    both = jnp.concatenate([t.reshape(-1, w) for t, w in zip(turned, widths)], axis=1)
    out = lax.all_gather(both, axis, axis=0, tiled=True)
    parts = jnp.split(out, [sum(widths[:k]) for k in range(1, len(widths))], axis=1)
    return tuple(
        (
            jnp.moveaxis(b.reshape(-1, *t.shape[1:]), 0, dim)
            for b, t, dim in zip(parts, turned, dims)
        )
    )


def body(
    train_query,
    low_query,
    high_query,
    train_key,
    low_key,
    high_key,
    train_value,
    low_value,
    high_value,
    train_mixed,
    low_mixed,
    high_mixed,
    norm_train,
    norm_step,
):
    result_query = train_query.astype(jnp.float32) + mix_rate * jnp.dot(
        low_query, high_query, preferred_element_type=jnp.float32
    )
    result_key = train_key.astype(jnp.float32) + mix_rate * jnp.dot(
        low_key, high_key, preferred_element_type=jnp.float32
    )
    result_value = train_value.astype(jnp.float32) + mix_rate * jnp.dot(
        low_value, high_value, preferred_element_type=jnp.float32
    )
    result_mixed = train_mixed.astype(jnp.float32) + mix_rate * jnp.dot(
        low_mixed, high_mixed, preferred_element_type=jnp.float32
    )
    narrow_query, narrow_key, narrow_value, narrow_mixed = (
        result_query.astype(jnp.bfloat16),
        result_key.astype(jnp.bfloat16),
        result_value.astype(jnp.bfloat16),
        result_mixed.astype(jnp.bfloat16),
    )
    final_query, final_key, final_value, final_mixed = rows_first(
        (narrow_query, narrow_key, narrow_value, narrow_mixed), "shard", (0, 0, 0, 1)
    )
    serve_norm = lax.all_gather(
        (norm_train + norm_step).astype(jnp.bfloat16), ("shard", "tp"), axis=0, tiled=True
    )
    return (final_query, final_key, final_value, final_mixed, serve_norm)


def solution(mesh):
    return jax.shard_map(
        body,
        mesh=mesh,
        in_specs=(
            P("shard", "tp"),
            P("shard", None),
            P(None, "tp"),
            P("shard", "tp"),
            P("shard", None),
            P(None, "tp"),
            P("shard", "tp"),
            P("shard", None),
            P(None, "tp"),
            P("tp", "shard"),
            P("tp", None),
            P(None, "shard"),
            P(("shard", "tp")),
            P(("shard", "tp")),
        ),
        out_specs=(P(None, "tp"), P(None, "tp"), P(None, "tp"), P("tp", None), P()),
        check_vma=False,
    )
```

profile of v0, /device:TPU:1, one launch (start us, length us, event | category | flops | bytes accessed | tf_op | source)
XLA Modules:
  0.0 198.9 jit_solution(14225677418639521225)
XLA Ops:
  7.2 0.0 copy-start
  7.2 0.0 copy-start.4
  7.2 0.0 copy-start.6
  7.2 0.0 copy-start.2
  7.2 0.0 copy-start.5
  7.2 0.0 copy-start.3
  7.2 0.0 copy-start.1
  7.2 0.0 all-gather.2.cloned.1.call-start
  7.3 0.7 copy-done
  8.0 1.5 fusion.4
  9.5 1.1 fusion.8
  10.6 0.0 copy-done.4
  10.7 0.2 fusion.7
  10.9 0.4 fusion.2
  11.3 1.2 pad_maximum_fusion
  12.5 0.0 all-gather.2.cloned.1.call-update
  12.5 0.6 copy-done.7
  13.1 0.0 copy-done.8
  13.2 0.2 dynamic-update-slice
  13.4 139.6 %all-reduce = bf16[5120]{0:T(1024)(128)(2,1)} all-reduce(bf16[5120]{0:T(1024)(128)(2,1)S(1)} %dynamic-update-slice), channel_id=1, replica_groups=mesh['shard'=16,'tp'=8] {'shard','tp'}, use_global_device_ids=true, to_apply=%add | all-reduce | flops 5120 | bytes 20480
  153.0 5.9 %all-gather.2.cloned.1.call-done = bf16[5120,2304]{1,0:T(8,128)(2,1)} async-done(((bf16[320,2304]{1,0:T(8,128)(2,1)}), bf16[5120,2304]{1,0:T(8,128)(2,1)}) %all-gather.2.cloned.1.call-update) | async-done | bytes 23592976 | tf_op jit(solution)/shard_map/all_gather | solution.py:13
  158.8 16.2 %slice_bitcast_fusion = (bf16[1024,5120]{0,1:T(8,128)(2,1)}, bf16[5120,1024]{1,0:T(8,128)(2,1)}) fusion(bf16[5120,2304]{1,0:T(8,128)(2,1)} %all-gather.2.cloned.1.call-done), kind=kLoop, calls=%fused_computation | loop fusion | bytes 41943040 | tf_op jit(solution)/shard_map/transpose | solution.py:17
  175.0 13.7 %copy.19 = bf16[1024,5120]{1,0:T(8,128)(2,1)} copy(bf16[1024,5120]{0,1:T(8,128)(2,1)} %get-tuple-element.10) | data formatting | bytes 20971520
  188.7 3.4 %fusion.9 = (bf16[5120,128]{1,0:T(8,128)(2,1)}, bf16[5120,128]{1,0:T(8,128)(2,1)}) fusion(bf16[5120,2304]{1,0:T(8,128)(2,1)} %all-gather.2.cloned.1.call-done), kind=kLoop, calls=%fused_computation.16 | loop fusion | bytes 5242880 | tf_op jit(solution)/shard_map/split | solution.py:14
  (9 shorter events, 0.0 us)
Async XLA Ops:
  7.2 0.8 copy-start
  7.2 3.4 %copy-start.4 = (bf16[320,32]{0,1:T(8,128)(2,1)S(1)}, bf16[320,32]{0,1:T(8,128)(2,1)}, u32[]{:S(2)}) copy-start(bf16[320,32]{0,1:T(8,128)(2,1)} %param.18) | copy-start | bytes 61444
  7.2 3.4 %copy-start.6 = (bf16[32,128]{1,0:T(8,128)(2,1)S(1)}, bf16[32,128]{1,0:T(8,128)(2,1)}, u32[]{:S(2)}) copy-start(bf16[32,128]{1,0:T(8,128)(2,1)} %param.19) | copy-start | bytes 24580
  7.2 3.4 %copy-start.2 = (bf16[320,128]{1,0:T(8,128)(2,1)S(1)}, bf16[320,128]{1,0:T(8,128)(2,1)}, u32[]{:S(2)}) copy-start(bf16[320,128]{1,0:T(8,128)(2,1)} %param.17) | copy-start | bytes 245764
  7.2 3.7 %copy-start.5 = (bf16[320,32]{0,1:T(8,128)(2,1)S(1)}, bf16[320,32]{0,1:T(8,128)(2,1)}, u32[]{:S(2)}) copy-start(bf16[320,32]{0,1:T(8,128)(2,1)} %param.15) | copy-start | bytes 61444
  7.2 3.7 %copy-start.3 = (bf16[32,1024]{1,0:T(8,128)(2,1)S(1)}, bf16[32,1024]{1,0:T(8,128)(2,1)}, u32[]{:S(2)}) copy-start(bf16[32,1024]{1,0:T(8,128)(2,1)} %param.16) | copy-start | bytes 196612
  7.2 3.7 %copy-start.1 = (bf16[320,1024]{1,0:T(8,128)(2,1)S(1)}, bf16[320,1024]{1,0:T(8,128)(2,1)}, u32[]{:S(2)}) copy-start(bf16[320,1024]{1,0:T(8,128)(2,1)} %param.14) | copy-start | bytes 1966084
  7.2 151.6 %all-gather.2.cloned.1.call-start = ((), (), s32[]{:S(2)}) async-start(), calls=%async_computation | async-start | bytes 25067520 | tf_op jit(solution)/shard_map/all_gather | solution.py:13
  12.5 0.7 copy-start.7
  12.5 0.7 copy-start.8
Sparse Core Ops, SparseCore 0:
  12.6 146.1 all-gather.1
where the time goes:
time: 200 us; the launch traced here: 199 us
  blocking collectives  140 us (70%)
  local copies, waits for them, and re-layouts  34.9 us (17%)
  between operations  14.2 us (7%)
  waiting for transfers between devices  5.87 us (3%)
  matrix products  3.16 us (2%)
    unnamed x1, blocking collectives  140 us
    transpose x1, local copies, waits for them, and re-layouts, rows_first(): jnp.moveaxis(b.reshape(-1, *t.shape[1:]), 0, dim)  16.2 us
    unnamed x21, local copies, waits for them, and re-layouts  15.3 us
    all_gather x1, waiting for transfers between devices, rows_first(): out = lax.all_gather(both, axis, axis=0, tiled=True)  5.85 us
  transfers between devices with their start and end apart: 1, of which 1 were waited for; matrix products, arithmetic and copies ran while one was open for 0% of the time, Pallas kernels for 0%

commit v1 on v0

--- a/solution.py
+++ b/solution.py
@@ -10,7 +10,15 @@
     turned = [jnp.moveaxis(a, dim, 0) for a, dim in zip(arrays, dims)]
     widths = [t[0].size for t in turned]
     both = jnp.concatenate([t.reshape(-1, w) for t, w in zip(turned, widths)], axis=1)
-    out = lax.all_gather(both, axis, axis=0, tiled=True)
+    out = jnp.concatenate(
+        jax.lax.all_to_all(
+            jnp.stack([both for _ in range(jax.lax.axis_size(axis))]),
+            axis_name=axis,
+            split_axis=0,
+            concat_axis=0,
+        ),
+        axis=0,
+    )
     parts = jnp.split(out, [sum(widths[:k]) for k in range(1, len(widths))], axis=1)
     return tuple(
         (

time: 200 us -> 427 us (2.13)
  blocking collectives: 140 us -> 371 us
  between operations: 14.2 us -> 0.8 us
  starting transfers between devices: 0.04 us -> 9.25 us
  local copies, waits for them, and re-layouts: 34.9 us -> 42.5 us
  waiting for transfers between devices: 5.87 us -> 0.01 us
    unnamed x1, blocking collectives: 140 us -> 371 us
    all_to_all x0 -> x1, starting transfers between devices: none -> 9.25 us  [rows_first(): jax.lax.all_to_all(jnp.stack([both for _ in range(jax.lax.axis_size(axis)...]
    another operation x0 -> x1, local copies, waits for them, and re-layouts: none -> 8.11 us  [rows_first(): jnp.stack([both for _ in range(jax.lax.axis_size(axis))])]
    all_gather x1 -> x0, waiting for transfers between devices: 5.85 us -> none  [rows_first(): out = lax.all_gather(both, axis, axis=0, tiled=True)]
    unnamed x21 -> x23, local copies, waits for them, and re-layouts: 15.3 us -> 14.8 us
  transfers between devices with their start and end apart: 1 -> 1, of which waited for: 1 -> 0; matrix products, arithmetic and copies ran while one was open for 0% -> 0% of each run, Pallas kernels for 0% -> 0%
where the time goes in v1:
time: 427 us
  blocking collectives  371 us (87%)
  local copies, waits for them, and re-layouts  42.5 us (10%)
  starting transfers between devices  9.25 us (2%)
    unnamed x1, blocking collectives  371 us
    transpose x1, local copies, waits for them, and re-layouts, rows_first(): jnp.moveaxis(b.reshape(-1, *t.shape[1:]), 0, dim)  16.2 us
    unnamed x23, local copies, waits for them, and re-layouts  14.8 us
    all_to_all x1, starting transfers between devices, rows_first(): jax.lax.all_to_all(jnp.stack([both for _ in range(jax.lax.axis_size(axis)...  9.25 us
  transfers between devices with their start and end apart: 1, of which 0 were waited for; matrix products, arithmetic and copies ran while one was open for 0% of the time, Pallas kernels for 0%

profile of v1, /device:TPU:1, one launch (start us, length us, event | category | flops | bytes accessed | tf_op | source)
XLA Modules:
  0.0 426.7 jit_solution(4948037981632056475)
XLA Ops:
  0.6 0.0 copy-start
  0.7 0.0 copy-start.5
  0.7 0.0 copy-start.7
  0.7 0.0 copy-start.3
  0.7 0.0 copy-start.6
  0.7 0.0 copy-start.4
  0.7 0.0 copy-start.2
  0.7 0.8 copy-done
  1.5 1.5 fusion.4
  3.0 1.1 fusion.8
  4.1 0.0 copy-done.5
  4.1 0.0 copy-done.7
  4.1 0.0 copy-done.3
  4.1 0.2 fusion.7
  4.4 0.4 fusion.2
  4.7 0.1 pad_maximum_fusion
  4.8 8.1 %stack.2 = bf16[16,320,2304]{2,1,0:T(8,128)(2,1)} broadcast(bf16[320,2304]{1,0:T(8,128)(2,1)S(1)} %pad_maximum_fusion), dimensions={1,2} | broadcast | bytes 25067520 | tf_op jit(solution)/shard_map/stack | solution.py:15
  13.0 9.3 %all-to-all-start = ((bf16[16,320,2304]{2,1,0:T(8,128)(2,1)}), bf16[16,320,2304]{2,1,0:T(8,128)(2,1)}, u32[]{:S(2)}, u32[]{:S(2)}) async-start(bf16[16,320,2304]{2,1,0:T(8,128)(2,1)} %stack.2), calls=%async_computation | async-start | bytes 47185920 | tf_op jit(solution)/shard_map/all_to_all | solution.py:14
  22.2 0.2 dynamic-update-slice
  22.5 370.9 %all-reduce = bf16[5120]{0:T(1024)(128)(2,1)} all-reduce(bf16[5120]{0:T(1024)(128)(2,1)S(1)} %dynamic-update-slice), channel_id=1, replica_groups=mesh['shard'=16,'tp'=8] {'shard','tp'}, use_global_device_ids=true, to_apply=%add | all-reduce | flops 5120 | bytes 20480
  393.4 0.0 all-to-all-done
  393.4 16.2 %slice_bitcast_fusion = (bf16[1024,5120]{0,1:T(8,128)(2,1)}, bf16[5120,1024]{1,0:T(8,128)(2,1)}) fusion(bf16[5120,2304]{1,0:T(8,128)(2,1)} %bitcast.1), kind=kLoop, calls=%fused_computation | loop fusion | bytes 41943040 | tf_op jit(solution)/shard_map/transpose | solution.py:25
  409.6 3.4 fusion.9
  413.0 13.7 %copy.23 = bf16[1024,5120]{1,0:T(8,128)(2,1)} copy(bf16[1024,5120]{0,1:T(8,128)(2,1)} %get-tuple-element.15) | data formatting | bytes 20971520
  (11 shorter events, 0.0 us)
Async XLA Ops:
  0.6 0.8 copy-start
  0.7 3.4 copy-start.5
  0.7 3.4 copy-start.7
  0.7 3.4 copy-start.3
  0.7 3.7 copy-start.6
  0.7 3.7 copy-start.4
  0.7 3.7 copy-start.2
  12.9 9.3 %copy-start.8 = (f32[40]{0:T(128)S(1)}, f32[40]{0:T(128)}, u32[]{:S(2)}) copy-start(f32[40]{0:T(128)} %param.26) | copy-start | bytes 484
  12.9 9.3 %copy-start.9 = (f32[40]{0:T(128)S(1)}, f32[40]{0:T(128)}, u32[]{:S(2)}) copy-start(f32[40]{0:T(128)} %param.27) | copy-start | bytes 484
  13.0 380.4 %all-to-all-start = ((bf16[16,320,2304]{2,1,0:T(8,128)(2,1)}), bf16[16,320,2304]{2,1,0:T(8,128)(2,1)}, u32[]{:S(2)}, u32[]{:S(2)}) async-start(bf16[16,320,2304]{2,1,0:T(8,128)(2,1)} %stack.2), calls=%async_computation | async-start | bytes 47185920 | tf_op jit(solution)/shard_map/all_to_all | solution.py:14
  413.0 13.7 %copy-start.1 = (bf16[1024,32]{0,1:T(8,128)(2,1)S(1)}, bf16[1024,32]{0,1:T(8,128)(2,1)}, u32[]{:S(2)}) copy-start(bf16[1024,32]{0,1:T(8,128)(2,1)} %param.24) | copy-start | bytes 196612
